TPU v7x, 256 devices: a whole 4x4x8 slice. The times are simulated.
256 devices in a mesh: snap: 8 (over z), vert: 32 (over x, y, core).
Axes of the slice: x: 4, y: 4, z: 8, core: 2. Of those that a mesh axis runs over, the one named last changes fastest.
Arguments:
- features: bfloat16 [16, 65536, 256], P('snap', 'vert'), may hold values from -6 to 6
- tile_rows: int32 [16, 2048], P('snap', 'vert'), may hold values from 0 to 15
- tile_cols: int32 [16, 2048], P('snap', 'vert'), may hold values from 0 to 21
- tile_vals: bfloat16 [16, 2048, 128, 128], P('snap', 'vert'), may hold values from -0.25 to 0.25
- send_lists: int32 [32, 6], replicated, may hold values from 0 to 15
- conv1_weight: bfloat16 [256, 256], replicated, may hold values from -0.375 to 0.375
- conv2_weight: bfloat16 [256, 256], replicated, may hold values from -0.375 to 0.375
- lstm_weight: bfloat16 [2, 512, 1024], replicated, may hold values from -0.25 to 0.25
- lstm_bias: float32 [2, 1024], replicated, may hold values from -4 to 4
Outputs:
- mixed: bfloat16 [16, 65536, 256], P('snap', 'vert')
All inputs are finite; a program needn't handle non-finite values.
Results may differ from a plain program's by a relative error of at most 0.007.
Values may be sent and summed in bfloat16 or wider, within the bound.
A program may use at most 128 MiB of HBM per device.

v0:
```python
import jax
import jax.numpy as jnp
from jax import lax
from jax.sharding import PartitionSpec as P

BS = 128


def with_halo(block, sides, width):
    for axis, dim in sides:
        count = lax.axis_size(axis)
        forward = [(i, i + 1) for i in range(count - 1)]
        forward.append((count - 1, 0))
        backward = [(target, source) for source, target in forward]
        low = lax.ppermute(
            lax.slice_in_dim(block, block.shape[dim] - width, None, axis=dim), axis, forward
        )
        high = lax.ppermute(lax.slice_in_dim(block, 0, width, axis=dim), axis, backward)
        block = jnp.concatenate([low, block, high], axis=dim)
    return block


def rims(packed, width):
    return with_halo(packed, (("vert", 1),), width)


def extend(field, send_lists, tile_cols):
    snapshots, vertices, width = field.shape
    blocks = vertices // BS
    bound = send_lists.shape[1] // 2
    device = lax.axis_index("vert")
    own_list = lax.dynamic_index_in_dim(send_lists, device, 0, keepdims=False)
    packed = jnp.take(field.reshape(snapshots, blocks, BS, width), own_list, axis=1).reshape(
        snapshots, 2 * bound * BS, width
    )
    bordered = rims(packed, bound * BS)
    extended = jnp.concatenate(
        [bordered[:, : bound * BS], field, bordered[:, bordered.shape[1] - bound * BS :]], axis=1
    )
    return (extended.reshape(snapshots, -1, BS, width), tile_cols)


def convolve(field, tile_rows, tile_cols, tile_vals, send_lists):
    snapshots, vertices, width = field.shape
    blocks = vertices // BS
    extended, position = extend(field, send_lists, tile_cols)
    picked = jax.vmap(lambda slab, where_at: jnp.take(slab, where_at, axis=0))(extended, position)
    product = jnp.einsum("skij,skjf->skif", tile_vals, picked, preferred_element_type=jnp.float32)
    onehot = (tile_rows[..., None] == jnp.arange(blocks, dtype=jnp.int32)).astype(jnp.float32)
    summed = jnp.einsum("skb,skif->sbif", onehot, product, preferred_element_type=jnp.float32)
    return summed.reshape(snapshots, vertices, width)


def project(field, weight):
    snapshots, vertices, width = field.shape
    result = jnp.dot(
        field.reshape(snapshots * vertices, width), weight, preferred_element_type=jnp.float32
    )
    return result.astype(jnp.bfloat16).reshape(snapshots, vertices, width)


def cell_step(inputs, hidden, memory, weight, bias):
    gates = (
        jnp.dot(
            jnp.concatenate([inputs, hidden], axis=-1), weight, preferred_element_type=jnp.float32
        )
        + bias
    )
    in_gate, forget, candidate, out_gate = jnp.split(gates, 4, axis=-1)
    memory = jax.nn.sigmoid(forget) * memory + jax.nn.sigmoid(in_gate) * jnp.tanh(candidate)
    hidden = (jax.nn.sigmoid(out_gate) * jnp.tanh(memory)).astype(jnp.bfloat16)
    return (hidden, memory)


def shards(
    features,
    tile_rows,
    tile_cols,
    tile_vals,
    send_lists,
    conv1_weight,
    conv2_weight,
    lstm_weight,
    lstm_bias,
):
    snapshots, vertices, width = features.shape
    projected = project(features, conv1_weight)
    convolved = jnp.maximum(
        convolve(projected, tile_rows, tile_cols, tile_vals, send_lists), 0.0
    ).astype(jnp.bfloat16)
    groups = lax.axis_size("snap")
    grouped = convolved.reshape(snapshots, groups, vertices // groups, width)
    sequence = lax.all_to_all(grouped, "snap", split_axis=1, concat_axis=0, tiled=True)[:, 0]
    count = sequence.shape[1]
    zero_h = jnp.zeros((count, width), jnp.bfloat16)
    zero_c = jnp.zeros((count, width), jnp.float32)

    def advance(carry, inputs):
        first_h, first_c, second_h, second_c = carry
        first_h, first_c = cell_step(inputs, first_h, first_c, lstm_weight[0], lstm_bias[0])
        second_h, second_c = cell_step(first_h, second_h, second_c, lstm_weight[1], lstm_bias[1])
        return ((first_h, first_c, second_h, second_c), second_h)

    carry, outputs = lax.scan(advance, (zero_h, zero_c, zero_h, zero_c), sequence)
    recurrent = outputs[:, None]
    restored = lax.all_to_all(recurrent, "snap", split_axis=0, concat_axis=1, tiled=True).reshape(
        snapshots, vertices, width
    )
    second = project(restored, conv2_weight)
    return convolve(second, tile_rows, tile_cols, tile_vals, send_lists).astype(jnp.bfloat16)


def solution(mesh):
    placed = (
        P("snap", "vert", None),
        P("snap", "vert"),
        P("snap", "vert"),
        P("snap", "vert", None, None),
        P(),
        P(),
        P(),
        P(),
        P(),
    )
    return jax.shard_map(
        shards, mesh=mesh, in_specs=placed, out_specs=P("snap", "vert", None), check_vma=False
    )
```

profile of v0, /device:TPU:31, one launch (start us, length us, event | category | flops | bytes accessed | tf_op | source)
XLA Modules:
  0.0 305.9 jit_solution(4708403883143465019)
XLA Ops:
  0.0 1.0 dynamic-slice_reduce_fusion
  1.6 2.9 convolution_convert_fusion.1
  4.5 2.2 gather_fusion
  7.0 2.2 collective-permute-start
  9.3 4.6 %collective-permute-done = bf16[2,384,256]{2,1,0:T(8,128)(2,1)S(1)} collective-permute-done((bf16[2,384,256]{2,1,0:T(8,128)(2,1)S(1)}, bf16[2,384,256]{2,1,0:T(8,128)(2,1)S(1)}, u32[]{:S(2)}, u32[]{:S(2)}) %collective-permute-start) | collective-permute-done | bytes 393248 | tf_op jit(solution)/shard_map/ppermute | solution.py:15
  13.9 5.8 %collective-permute-done.1 = bf16[2,384,256]{2,1,0:T(8,128)(2,1)S(1)} collective-permute-done((bf16[2,384,256]{2,1,0:T(8,128)(2,1)S(1)}, bf16[2,384,256]{2,1,0:T(8,128)(2,1)S(1)}, u32[]{:S(2)}, u32[]{:S(2)}) %collective-permute-start.1) | collective-permute-done | bytes 393248 | tf_op jit(solution)/shard_map/ppermute | solution.py:18
  20.5 1.9 pad_maximum_fusion
  22.4 7.2 %gather_fusion.1 = bf16[128,128,256]{2,1,0:T(8,128)(2,1)} fusion(bf16[2,22,128,256]{3,2,1,0:T(8,128)(2,1)S(1)} %bitcast.76, s32[128]{0:T(128)S(1)} %reshape.92), kind=kCustom, calls=%fused_computation.1.clone | custom fusion | bytes 16778240 | tf_op jit(solution)/shard_map/vmap(jit(_take))/gather | solution.py:47
  29.6 12.0 %copy.35 = bf16[2,64,128,256]{2,3,1,0:T(8,128)(2,1)} copy(bf16[2,64,128,256]{3,2,1,0:T(8,128)(2,1)} %bitcast.78) | data formatting | bytes 16777216 | tf_op jit(solution)/shard_map/vmap(jit(_take))/gather | solution.py:47
  41.6 11.6 %fusion.46 = bf16[2,64,128,256]{2,3,1,0:T(8,128)(2,1)} fusion(bf16[2,64,128,128]{3,2,1,0:T(8,128)(2,1)} %param.18, bf16[2,64,128,256]{2,3,1,0:T(8,128)(2,1)} %copy.35, pred[2,64]{1,0:T(4,128)(4,1)S(1)} %compare_and_fusion), kind=kOutput, calls=%fused_computation.64 | convolution fusion | flops 1077936128 | bytes 20971648 | tf_op jit(solution)/shard_map/skij,skjf->skif/dot_general | solution.py:48
  53.2 12.3 %copy.36 = bf16[2,64,128,256]{3,1,2,0:T(8,128)(2,1)} copy(bf16[2,64,128,256]{2,3,1,0:T(8,128)(2,1)} %fusion.46) | data formatting | bytes 16777216 | tf_op jit(solution)/shard_map/skij,skjf->skif/dot_general | solution.py:48
  65.5 4.6 %maximum_convert_fusion = bf16[2,16,128,256]{3,1,2,0:T(8,128)(2,1)S(1)} fusion(bf16[2,64,128,256]{3,1,2,0:T(8,128)(2,1)} %copy.36, s32[2,64]{1,0:T(2,128)S(1)} %copy-done.6), kind=kOutput, calls=%fused_computation.70 | convolution fusion | flops 137365504 | bytes 10486272 | tf_op jit(solution)/shard_map/skb,skif->sbif/dot_general | solution.py:50
  70.9 1.5 copy.38
  72.4 6.5 %all-to-all-start = ((bf16[2,8,256,256]{3,2,0,1:T(8,128)(2,1)}), bf16[2,8,256,256]{3,2,0,1:T(8,128)(2,1)S(1)}, u32[]{:S(2)}, u32[]{:S(2)}) async-start(bf16[2,8,256,256]{3,2,0,1:T(8,128)(2,1)} %copy.38), calls=%async_computation | async-start | bytes 4194304 | tf_op jit(solution)/shard_map/all_to_all | solution.py:93
  78.9 49.3 %all-to-all-done = bf16[2,8,256,256]{3,2,0,1:T(8,128)(2,1)S(1)} async-done(((bf16[2,8,256,256]{3,2,0,1:T(8,128)(2,1)}), bf16[2,8,256,256]{3,2,0,1:T(8,128)(2,1)S(1)}, u32[]{:S(2)}, u32[]{:S(2)}) %all-to-all-start) | async-done | bytes 2097184 | tf_op jit(solution)/shard_map/all_to_all | solution.py:93
  128.2 57.3 %while.19 = (s32[]{:T(128)}, bf16[256,256]{1,0:T(8,128)(2,1)S(1)}, f32[256,256]{1,0:T(8,128)S(1)}, bf16[256,256]{1,0:T(8,128)(2,1)S(1)}, f32[256,256]{1,0:T(8,12...) while((s32[]{:T(128)}, bf16[256,256]{1,0:T(8,128)(2,1)S(1)}, ...), condition=%wide.region_1.4_spmd.clone, body=%wide.region_0.0_spmd.clone.sunk | while | flops 540540928 | bytes 17457816 | solution.py:104
  128.3 1.8 convolution_add_fusion.4
  131.9 1.8 convolution_add_fusion.4
  134.4 0.9 bitcast_dynamic-update-slice_fusion.2
  135.5 1.8 convolution_add_fusion.4
  138.0 0.9 bitcast_dynamic-update-slice_fusion.2
  139.0 1.8 convolution_add_fusion.4
  141.6 0.9 bitcast_dynamic-update-slice_fusion.2
  142.6 1.8 convolution_add_fusion.4
  145.2 0.9 bitcast_dynamic-update-slice_fusion.2
  146.2 1.8 convolution_add_fusion.4
  148.8 0.9 bitcast_dynamic-update-slice_fusion.2
  149.8 1.8 convolution_add_fusion.4
  153.4 1.8 convolution_add_fusion.4
  157.0 1.8 convolution_add_fusion.4
  160.5 1.8 convolution_add_fusion.4
  164.1 1.8 convolution_add_fusion.4
  167.7 1.8 convolution_add_fusion.4
  171.3 1.8 convolution_add_fusion.4
  174.9 1.8 convolution_add_fusion.4
  178.5 1.8 convolution_add_fusion.4
  182.0 1.8 convolution_add_fusion.4
  185.6 54.9 %all_to_all.30 = bf16[16,1,256,256]{3,2,1,0:T(8,128)(2,1)S(1)} all-to-all(bf16[16,1,256,256]{3,2,1,0:T(8,128)(2,1)} %bitcast.89), channel_id=1, replica_groups=mesh['snap'=8,'vert'=32] {'snap'}, dimensions={0} | all-to-all | bytes 4194304 | tf_op jit(solution)/shard_map/all_to_all | solution.py:106
  242.3 1.4 collective-permute-start.2
  243.7 4.7 %collective-permute-done.2 = bf16[2,384,256]{2,1,0:T(8,128)(2,1)S(1)} collective-permute-done((bf16[2,384,256]{2,1,0:T(8,128)(2,1)S(1)}, bf16[2,384,256]{2,1,0:T(8,128)(2,1)S(1)}, u32[]{:S(2)}, u32[]{:S(2)}) %collective-permute-start.2) | collective-permute-done | bytes 393248 | tf_op jit(solution)/shard_map/ppermute | solution.py:15
  248.4 5.8 %collective-permute-done.3 = bf16[2,384,256]{2,1,0:T(8,128)(2,1)S(1)} collective-permute-done((bf16[2,384,256]{2,1,0:T(8,128)(2,1)S(1)}, bf16[2,384,256]{2,1,0:T(8,128)(2,1)S(1)}, u32[]{:S(2)}, u32[]{:S(2)}) %collective-permute-start.3) | collective-permute-done | bytes 393248 | tf_op jit(solution)/shard_map/ppermute | solution.py:18
  254.2 1.8 pad_maximum_fusion.1
  256.0 7.2 %gather_fusion.3 = bf16[128,128,256]{2,1,0:T(8,128)(2,1)} fusion(bf16[2,22,128,256]{3,2,1,0:T(8,128)(2,1)S(1)} %bitcast.75, s32[128]{0:T(128)S(1)} %reshape.92), kind=kCustom, calls=%fused_computation.3.clone | custom fusion | bytes 16778240 | tf_op jit(solution)/shard_map/vmap(jit(_take))/gather | solution.py:47
  263.2 12.0 %copy.41 = bf16[2,64,128,256]{2,3,1,0:T(8,128)(2,1)} copy(bf16[2,64,128,256]{3,2,1,0:T(8,128)(2,1)} %bitcast.77) | data formatting | bytes 16777216 | tf_op jit(solution)/shard_map/vmap(jit(_take))/gather | solution.py:47
  275.2 11.6 %fusion.49 = bf16[2,64,128,256]{2,3,1,0:T(8,128)(2,1)} fusion(bf16[2,64,128,128]{3,2,1,0:T(8,128)(2,1)} %param.18, bf16[2,64,128,256]{2,3,1,0:T(8,128)(2,1)} %copy.41, pred[2,64]{1,0:T(4,128)(4,1)S(1)} %compare_and_fusion), kind=kOutput, calls=%fused_computation.65 | convolution fusion | flops 1077936128 | bytes 20971648 | tf_op jit(solution)/shard_map/skij,skjf->skif/dot_general | solution.py:48
  286.8 12.3 %copy.42 = bf16[2,64,128,256]{3,1,2,0:T(8,128)(2,1)} copy(bf16[2,64,128,256]{2,3,1,0:T(8,128)(2,1)} %fusion.49) | data formatting | bytes 16777216 | tf_op jit(solution)/shard_map/skij,skjf->skif/dot_general | solution.py:48
  299.1 4.7 %convolution_convert_fusion.2 = bf16[2,16,128,256]{3,1,2,0:T(8,128)(2,1)S(1)} fusion(bf16[2,64,128,256]{3,1,2,0:T(8,128)(2,1)} %copy.42, s32[2,64]{1,0:T(2,128)S(1)} %copy-done.6), kind=kOutput, calls=%fused_computation.73 | convolution fusion | flops 134219776 | bytes 10486272 | tf_op jit(solution)/shard_map/skb,skif->sbif/dot_general | solution.py:50
  303.8 2.1 copy.43
  (162 shorter events, 27.1 us)
Async XLA Ops:
  0.0 1.6 copy-start
  4.5 4.7 %copy-start.7 = (s32[2,64]{1,0:T(2,128)S(1)}, s32[2,64]{1,0:T(2,128)}, u32[]{:S(2)}) copy-start(s32[2,64]{1,0:T(2,128)} %param.17) | copy-start | bytes 1540
  7.0 6.9 %collective-permute-start = (bf16[2,384,256]{2,1,0:T(8,128)(2,1)S(1)}, bf16[2,384,256]{2,1,0:T(8,128)(2,1)S(1)}, u32[]{:S(2)}, u32[]{:S(2)}) collective-permute-start(bf16[2,384,256]{2,1,0:T(8,128)(2,1)S(1)} %get-tuple-element.114), channel_id=1, source_target_pairs={{0,1},{1,2},{2,3},{3,4},{4,5},{5,6},{6,7},{7,8},{8,9},{9,10},{10,1... | collective-permute-start | bytes 1179656 | tf_op jit(solution)/shard_map/ppermute | solution.py:15
  9.2 10.5 %collective-permute-start.1 = (bf16[2,384,256]{2,1,0:T(8,128)(2,1)S(1)}, bf16[2,384,256]{2,1,0:T(8,128)(2,1)S(1)}, u32[]{:S(2)}, u32[]{:S(2)}) collective-permute-start(bf16[2,384,256]{2,1,0:T(8,128)(2,1)S(1)} %get-tuple-element.115), channel_id=1, source_target_pairs={{1,0},{2,1},{3,2},{4,3},{5,4},{6,5},{7,6},{8,7},{9,8},{10,9},{11,1... | collective-permute-start | bytes 1179656 | tf_op jit(solution)/shard_map/ppermute | solution.py:18
  19.7 0.7 copy-start.3
  53.2 12.3 %copy-start.6 = (s32[2,64]{1,0:T(2,128)S(1)}, s32[2,64]{1,0:T(2,128)}, u32[]{:S(2)}) copy-start(s32[2,64]{1,0:T(2,128)} %param.16) | copy-start | bytes 1540
  70.9 57.3 %copy-start.4 = (f32[2,1024]{1,0:T(2,128)S(1)}, f32[2,1024]{1,0:T(2,128)}, u32[]{:S(2)}) copy-start(f32[2,1024]{1,0:T(2,128)} %param.23) | copy-start | bytes 24580
  72.4 55.8 %all-to-all-start = ((bf16[2,8,256,256]{3,2,0,1:T(8,128)(2,1)}), bf16[2,8,256,256]{3,2,0,1:T(8,128)(2,1)S(1)}, u32[]{:S(2)}, u32[]{:S(2)}) async-start(bf16[2,8,256,256]{3,2,0,1:T(8,128)(2,1)} %copy.38), calls=%async_computation | async-start | bytes 4194304 | tf_op jit(solution)/shard_map/all_to_all | solution.py:93
  128.2 2.2 copy-start.8
  131.8 2.2 copy-start.8
  135.4 2.2 copy-start.8
  139.0 2.2 copy-start.8
  142.6 2.2 copy-start.8
  146.1 2.2 copy-start.8
  149.7 2.2 copy-start.8
  153.3 2.2 copy-start.8
  156.9 2.2 copy-start.8
  160.5 2.2 copy-start.8
  164.1 2.2 copy-start.8
  167.6 2.2 copy-start.8
  171.2 2.2 copy-start.8
  174.8 2.2 copy-start.8
  178.4 2.2 copy-start.8
  182.0 2.2 copy-start.8
  185.6 55.1 %copy-start.5 = (bf16[256,256]{1,0:T(8,128)(2,1)S(1)}, bf16[256,256]{1,0:T(8,128)(2,1)}, u32[]{:S(2)}) copy-start(bf16[256,256]{1,0:T(8,128)(2,1)} %param.21) | copy-start | bytes 393220
  241.4 12.8 %copy-start.2 = (bf16[4096,256]{1,0:T(8,128)(2,1)}, bf16[4096,256]{1,0:T(8,128)(2,1)S(1)}, u32[]{:S(2)}) copy-start(bf16[4096,256]{1,0:T(8,128)(2,1)S(1)} %convolution_convert_fusion) | copy-start | bytes 6291460
  242.3 6.1 %collective-permute-start.2 = (bf16[2,384,256]{2,1,0:T(8,128)(2,1)S(1)}, bf16[2,384,256]{2,1,0:T(8,128)(2,1)S(1)}, u32[]{:S(2)}, u32[]{:S(2)}) collective-permute-start(bf16[2,384,256]{2,1,0:T(8,128)(2,1)S(1)} %get-tuple-element.112), channel_id=1, source_target_pairs={{0,1},{1,2},{2,3},{3,4},{4,5},{5,6},{6,7},{7,8},{8,9},{9,10},{10,1... | collective-permute-start | bytes 1179656 | tf_op jit(solution)/shard_map/ppermute | solution.py:15
  243.7 10.5 %collective-permute-start.3 = (bf16[2,384,256]{2,1,0:T(8,128)(2,1)S(1)}, bf16[2,384,256]{2,1,0:T(8,128)(2,1)S(1)}, u32[]{:S(2)}, u32[]{:S(2)}) collective-permute-start(bf16[2,384,256]{2,1,0:T(8,128)(2,1)S(1)} %get-tuple-element.113), channel_id=1, source_target_pairs={{1,0},{2,1},{3,2},{4,3},{5,4},{6,5},{7,6},{8,7},{9,8},{10,9},{11,1... | collective-permute-start | bytes 1179656 | tf_op jit(solution)/shard_map/ppermute | solution.py:18
  299.1 6.8 %copy-start.1 = (bf16[2,2048,256]{2,1,0:T(8,128)(2,1)S(1)}, bf16[2,2048,256]{2,1,0:T(8,128)(2,1)}, u32[]{:S(2)}) copy-start(bf16[2,2048,256]{2,1,0:T(8,128)(2,1)} %param.15) | copy-start | bytes 6291460
where the time goes:
time: 307 us; the launch traced here: 306 us
  local copies, waits for them, and re-layouts  73.4 us (24%)
  matrix products  72.1 us (23%)
  waiting for transfers between devices  70.3 us (23%)
  blocking collectives  54.9 us (18%)
  other arithmetic  24.2 us (8%)
  starting transfers between devices  10.1 us (3%)
    all_to_all x1, blocking collectives, shards(): lax.all_to_all(recurrent, 'snap', split_axis=0, concat_axis=1, tiled=True)  54.9 us
    all_to_all x1, waiting for transfers between devices, shards(): lax.all_to_all(grouped, 'snap', split_axis=1, concat_axis=0, tiled=True)  49.3 us
    gather x5, local copies, waits for them, and re-layouts, convolve(): jnp.take(slab, where_at, axis=0)  38.5 us
    dot_general x32, matrix products, cell_step(): jnp.dot(jnp.concatenate([inputs, hidden], axis=-1), weight, preferred_ele...  35.9 us
    dot_general x2, local copies, waits for them, and re-layouts, convolve(): jnp.einsum('skij,skjf->skif', tile_vals, picked, preferred_element_type=j...  24.5 us
    dot_general x2, matrix products, convolve(): jnp.einsum('skij,skjf->skif', tile_vals, picked, preferred_element_type=j...  23.2 us
    dynamic_update_slice x16, other arithmetic, shards(): lax.scan(advance, (zero_h, zero_c, zero_h, zero_c), sequence)  15.2 us
    ppermute x2, waiting for transfers between devices, with_halo(): lax.ppermute(lax.slice_in_dim(block, 0, width, axis=dim), axis, backward)  11.6 us
  transfers between devices with their start and end apart: 5, of which 5 were waited for; matrix products, arithmetic and copies ran while one was open for 0% of the time, Pallas kernels for 0%

commit v1 on v0

--- a/solution.py
+++ b/solution.py
@@ -103,9 +103,12 @@
 
     carry, outputs = lax.scan(advance, (zero_h, zero_c, zero_h, zero_c), sequence)
     recurrent = outputs[:, None]
-    restored = lax.all_to_all(recurrent, "snap", split_axis=0, concat_axis=1, tiled=True).reshape(
-        snapshots, vertices, width
-    )
+    restored = jnp.concatenate(
+        lax.all_to_all(
+            jnp.stack(jnp.split(recurrent, lax.axis_size("snap"), axis=0)), "snap", 0, 0
+        ),
+        axis=1,
+    ).reshape(snapshots, vertices, width)
     second = project(restored, conv2_weight)
     return convolve(second, tile_rows, tile_cols, tile_vals, send_lists).astype(jnp.bfloat16)
 

time: 307 us -> 312 us (1.016)
  local copies, waits for them, and re-layouts: 73.4 us -> 78.6 us
    unnamed x16 -> x25, local copies, waits for them, and re-layouts: 1.33 us -> 6.63 us
where the time goes in v1:
time: 312 us; the launch traced here: 311 us
  local copies, waits for them, and re-layouts  78.6 us (25%)
  matrix products  72.4 us (23%)
  waiting for transfers between devices  70.3 us (23%)
  blocking collectives  53.7 us (17%)
  other arithmetic  24.2 us (8%)
  starting transfers between devices  10.3 us (3%)
    all_to_all x1, blocking collectives, shards(): lax.all_to_all(jnp.stack(jnp.split(recurrent, lax.axis_size('snap'), axis...  53.7 us
    all_to_all x1, waiting for transfers between devices, shards(): lax.all_to_all(grouped, 'snap', split_axis=1, concat_axis=0, tiled=True)  49.3 us
    gather x5, local copies, waits for them, and re-layouts, convolve(): jnp.take(slab, where_at, axis=0)  38.5 us
    dot_general x32, matrix products, cell_step(): jnp.dot(jnp.concatenate([inputs, hidden], axis=-1), weight, preferred_ele...  36 us
    dot_general x2, local copies, waits for them, and re-layouts, convolve(): jnp.einsum('skij,skjf->skif', tile_vals, picked, preferred_element_type=j...  24.4 us
    dot_general x2, matrix products, convolve(): jnp.einsum('skij,skjf->skif', tile_vals, picked, preferred_element_type=j...  23.4 us
    dynamic_update_slice x16, other arithmetic, shards(): lax.scan(advance, (zero_h, zero_c, zero_h, zero_c), sequence)  15.2 us
    ppermute x2, waiting for transfers between devices, with_halo(): lax.ppermute(lax.slice_in_dim(block, 0, width, axis=dim), axis, backward)  11.6 us
  transfers between devices with their start and end apart: 5, of which 5 were waited for; matrix products, arithmetic and copies ran while one was open for 0% of the time, Pallas kernels for 0%

profile of v1, /device:TPU:31, one launch (start us, length us, event | category | flops | bytes accessed | tf_op | source)
XLA Modules:
  0.0 310.6 jit_solution(6708245566546643501)
XLA Ops:
  0.0 1.0 dynamic-slice_reduce_fusion
  1.6 2.9 convolution_convert_fusion.1
  4.5 2.2 gather_fusion
  7.0 2.2 collective-permute-start
  9.3 4.6 %collective-permute-done = bf16[2,384,256]{2,1,0:T(8,128)(2,1)S(1)} collective-permute-done((bf16[2,384,256]{2,1,0:T(8,128)(2,1)S(1)}, bf16[2,384,256]{2,1,0:T(8,128)(2,1)S(1)}, u32[]{:S(2)}, u32[]{:S(2)}) %collective-permute-start) | collective-permute-done | bytes 393248 | tf_op jit(solution)/shard_map/ppermute | solution.py:15
  13.9 5.8 %collective-permute-done.1 = bf16[2,384,256]{2,1,0:T(8,128)(2,1)S(1)} collective-permute-done((bf16[2,384,256]{2,1,0:T(8,128)(2,1)S(1)}, bf16[2,384,256]{2,1,0:T(8,128)(2,1)S(1)}, u32[]{:S(2)}, u32[]{:S(2)}) %collective-permute-start.1) | collective-permute-done | bytes 393248 | tf_op jit(solution)/shard_map/ppermute | solution.py:18
  20.5 1.9 pad_maximum_fusion
  22.4 7.2 %gather_fusion.1 = bf16[128,128,256]{2,1,0:T(8,128)(2,1)} fusion(bf16[2,22,128,256]{3,2,1,0:T(8,128)(2,1)S(1)} %bitcast.90, s32[128]{0:T(128)S(1)} %reshape.111), kind=kCustom, calls=%fused_computation.1.clone | custom fusion | bytes 16778240 | tf_op jit(solution)/shard_map/vmap(jit(_take))/gather | solution.py:47
  29.6 12.0 %copy.33 = bf16[2,64,128,256]{2,3,1,0:T(8,128)(2,1)} copy(bf16[2,64,128,256]{3,2,1,0:T(8,128)(2,1)} %bitcast.92) | data formatting | bytes 16777216 | tf_op jit(solution)/shard_map/vmap(jit(_take))/gather | solution.py:47
  41.6 11.7 %fusion.46 = bf16[2,64,128,256]{2,3,1,0:T(8,128)(2,1)} fusion(bf16[2,64,128,128]{3,2,1,0:T(8,128)(2,1)} %param.18, bf16[2,64,128,256]{2,3,1,0:T(8,128)(2,1)} %copy.33, pred[2,64]{1,0:T(4,128)(4,1)S(1)} %compare_and_fusion), kind=kOutput, calls=%fused_computation.64 | convolution fusion | flops 1077936128 | bytes 20971648 | tf_op jit(solution)/shard_map/skij,skjf->skif/dot_general | solution.py:48
  53.4 12.2 %copy.34 = bf16[2,64,128,256]{3,1,2,0:T(8,128)(2,1)} copy(bf16[2,64,128,256]{2,3,1,0:T(8,128)(2,1)} %fusion.46) | data formatting | bytes 16777216 | tf_op jit(solution)/shard_map/skij,skjf->skif/dot_general | solution.py:48
  65.6 4.6 %maximum_convert_fusion = bf16[2,16,128,256]{3,1,2,0:T(8,128)(2,1)S(1)} fusion(bf16[2,64,128,256]{3,1,2,0:T(8,128)(2,1)} %copy.34, s32[2,64]{1,0:T(2,128)S(1)} %copy-done.7), kind=kOutput, calls=%fused_computation.70 | convolution fusion | flops 137365504 | bytes 10486272 | tf_op jit(solution)/shard_map/skb,skif->sbif/dot_general | solution.py:50
  70.9 1.5 copy.36
  72.4 6.6 %all-to-all-start = ((bf16[2,8,256,256]{3,2,0,1:T(8,128)(2,1)}), bf16[2,8,256,256]{3,2,0,1:T(8,128)(2,1)S(1)}, u32[]{:S(2)}, u32[]{:S(2)}) async-start(bf16[2,8,256,256]{3,2,0,1:T(8,128)(2,1)} %copy.36), calls=%async_computation | async-start | bytes 4194304 | tf_op jit(solution)/shard_map/all_to_all | solution.py:93
  79.0 49.3 %all-to-all-done = bf16[2,8,256,256]{3,2,0,1:T(8,128)(2,1)S(1)} async-done(((bf16[2,8,256,256]{3,2,0,1:T(8,128)(2,1)}), bf16[2,8,256,256]{3,2,0,1:T(8,128)(2,1)S(1)}, u32[]{:S(2)}, u32[]{:S(2)}) %all-to-all-start) | async-done | bytes 2097184 | tf_op jit(solution)/shard_map/all_to_all | solution.py:93
  128.4 57.6 %while.19 = (s32[]{:T(128)}, bf16[256,256]{1,0:T(8,128)(2,1)S(1)}, f32[256,256]{1,0:T(8,128)S(1)}, bf16[256,256]{1,0:T(8,128)(2,1)S(1)}, f32[256,256]{1,0:T(8,12...) while((s32[]{:T(128)}, bf16[256,256]{1,0:T(8,128)(2,1)S(1)}, ...), condition=%wide.region_1.4_spmd.clone, body=%wide.region_0.0_spmd.clone.sunk | while | flops 540540928 | bytes 17457816 | solution.py:104
  128.5 1.8 convolution_add_fusion.4
  131.0 0.9 bitcast_dynamic-update-slice_fusion.10
  132.1 1.8 convolution_add_fusion.4
  135.7 1.8 convolution_add_fusion.4
  139.3 1.8 convolution_add_fusion.4
  142.9 1.8 convolution_add_fusion.4
  146.5 1.8 convolution_add_fusion.4
  150.1 1.8 convolution_add_fusion.4
  153.7 1.8 convolution_add_fusion.4
  157.3 1.8 convolution_add_fusion.4
  160.9 1.8 convolution_add_fusion.4
  164.5 1.8 convolution_add_fusion.4
  168.1 1.8 convolution_add_fusion.4
  171.7 1.8 convolution_add_fusion.4
  175.3 1.8 convolution_add_fusion.4
  178.9 1.8 convolution_add_fusion.4
  182.5 1.8 convolution_add_fusion.4
  186.0 1.1 bitcast_dynamic-update-slice_fusion.8
  187.1 1.0 bitcast_dynamic-update-slice_fusion.7
  188.1 1.0 bitcast_dynamic-update-slice_fusion.6
  189.1 1.0 bitcast_dynamic-update-slice_fusion.5
  190.2 53.7 %all_to_all.20 = bf16[8,2,1,256,256]{4,3,1,2,0:T(8,128)(2,1)S(1)} all-to-all(bf16[8,2,1,256,256]{4,3,1,2,0:T(8,128)(2,1)S(1)} %bitcast_dynamic-update-slice_fusion.1), channel_id=1, replica_groups=mesh['snap'=8,'vert'=32] {'snap'}, dimensions={0} | all-to-all | bytes 4194304 | tf_op jit(solution)/shard_map/all_to_all | solution.py:107
  246.9 1.4 collective-permute-start.2
  248.3 4.7 %collective-permute-done.2 = bf16[2,384,256]{2,1,0:T(8,128)(2,1)S(1)} collective-permute-done((bf16[2,384,256]{2,1,0:T(8,128)(2,1)S(1)}, bf16[2,384,256]{2,1,0:T(8,128)(2,1)S(1)}, u32[]{:S(2)}, u32[]{:S(2)}) %collective-permute-start.2) | collective-permute-done | bytes 393248 | tf_op jit(solution)/shard_map/ppermute | solution.py:15
  253.0 5.8 %collective-permute-done.3 = bf16[2,384,256]{2,1,0:T(8,128)(2,1)S(1)} collective-permute-done((bf16[2,384,256]{2,1,0:T(8,128)(2,1)S(1)}, bf16[2,384,256]{2,1,0:T(8,128)(2,1)S(1)}, u32[]{:S(2)}, u32[]{:S(2)}) %collective-permute-start.3) | collective-permute-done | bytes 393248 | tf_op jit(solution)/shard_map/ppermute | solution.py:18
  258.8 1.8 pad_maximum_fusion.1
  260.6 7.2 %gather_fusion.3 = bf16[128,128,256]{2,1,0:T(8,128)(2,1)} fusion(bf16[2,22,128,256]{3,2,1,0:T(8,128)(2,1)S(1)} %bitcast.89, s32[128]{0:T(128)S(1)} %reshape.111), kind=kCustom, calls=%fused_computation.3.clone | custom fusion | bytes 16778240 | tf_op jit(solution)/shard_map/vmap(jit(_take))/gather | solution.py:47
  267.8 12.0 %copy.39 = bf16[2,64,128,256]{2,3,1,0:T(8,128)(2,1)} copy(bf16[2,64,128,256]{3,2,1,0:T(8,128)(2,1)} %bitcast.91) | data formatting | bytes 16777216 | tf_op jit(solution)/shard_map/vmap(jit(_take))/gather | solution.py:47
  279.8 11.7 %fusion.49 = bf16[2,64,128,256]{2,3,1,0:T(8,128)(2,1)} fusion(bf16[2,64,128,128]{3,2,1,0:T(8,128)(2,1)} %param.18, bf16[2,64,128,256]{2,3,1,0:T(8,128)(2,1)} %copy.39, pred[2,64]{1,0:T(4,128)(4,1)S(1)} %compare_and_fusion), kind=kOutput, calls=%fused_computation.65 | convolution fusion | flops 1077936128 | bytes 20971648 | tf_op jit(solution)/shard_map/skij,skjf->skif/dot_general | solution.py:48
  291.6 12.2 %copy.40 = bf16[2,64,128,256]{3,1,2,0:T(8,128)(2,1)} copy(bf16[2,64,128,256]{2,3,1,0:T(8,128)(2,1)} %fusion.49) | data formatting | bytes 16777216 | tf_op jit(solution)/shard_map/skij,skjf->skif/dot_general | solution.py:48
  303.8 4.7 %convolution_convert_fusion.2 = bf16[2,16,128,256]{3,1,2,0:T(8,128)(2,1)S(1)} fusion(bf16[2,64,128,256]{3,1,2,0:T(8,128)(2,1)} %copy.40, s32[2,64]{1,0:T(2,128)S(1)} %copy-done.7), kind=kOutput, calls=%fused_computation.73 | convolution fusion | flops 134219776 | bytes 10486272 | tf_op jit(solution)/shard_map/skb,skif->sbif/dot_general | solution.py:50
  308.5 2.1 copy.41
  (172 shorter events, 32.3 us)
Async XLA Ops:
  0.0 1.6 copy-start
  6.7 2.5 copy-start.8
  7.0 6.9 %collective-permute-start = (bf16[2,384,256]{2,1,0:T(8,128)(2,1)S(1)}, bf16[2,384,256]{2,1,0:T(8,128)(2,1)S(1)}, u32[]{:S(2)}, u32[]{:S(2)}) collective-permute-start(bf16[2,384,256]{2,1,0:T(8,128)(2,1)S(1)} %get-tuple-element.114), channel_id=1, source_target_pairs={{0,1},{1,2},{2,3},{3,4},{4,5},{5,6},{6,7},{7,8},{8,9},{9,10},{10,1... | collective-permute-start | bytes 1179656 | tf_op jit(solution)/shard_map/ppermute | solution.py:15
  9.2 10.5 %collective-permute-start.1 = (bf16[2,384,256]{2,1,0:T(8,128)(2,1)S(1)}, bf16[2,384,256]{2,1,0:T(8,128)(2,1)S(1)}, u32[]{:S(2)}, u32[]{:S(2)}) collective-permute-start(bf16[2,384,256]{2,1,0:T(8,128)(2,1)S(1)} %get-tuple-element.115), channel_id=1, source_target_pairs={{1,0},{2,1},{3,2},{4,3},{5,4},{6,5},{7,6},{8,7},{9,8},{10,9},{11,1... | collective-permute-start | bytes 1179656 | tf_op jit(solution)/shard_map/ppermute | solution.py:18
  19.7 0.8 copy-start.4
  53.3 12.2 %copy-start.7 = (s32[2,64]{1,0:T(2,128)S(1)}, s32[2,64]{1,0:T(2,128)}, u32[]{:S(2)}) copy-start(s32[2,64]{1,0:T(2,128)} %param.16) | copy-start | bytes 1540
  72.4 56.0 %copy-start.5 = (f32[2,1024]{1,0:T(2,128)S(1)}, f32[2,1024]{1,0:T(2,128)}, u32[]{:S(2)}) copy-start(f32[2,1024]{1,0:T(2,128)} %param.23) | copy-start | bytes 24580
  72.4 56.0 %all-to-all-start = ((bf16[2,8,256,256]{3,2,0,1:T(8,128)(2,1)}), bf16[2,8,256,256]{3,2,0,1:T(8,128)(2,1)S(1)}, u32[]{:S(2)}, u32[]{:S(2)}) async-start(bf16[2,8,256,256]{3,2,0,1:T(8,128)(2,1)} %copy.36), calls=%async_computation | async-start | bytes 4194304 | tf_op jit(solution)/shard_map/all_to_all | solution.py:93
  128.4 2.1 copy-start.9
  132.0 2.1 copy-start.9
  135.6 2.1 copy-start.9
  139.2 2.1 copy-start.9
  142.8 2.1 copy-start.9
  146.4 2.1 copy-start.9
  150.0 2.1 copy-start.9
  153.6 2.1 copy-start.9
  157.2 2.1 copy-start.9
  160.8 2.1 copy-start.9
  164.4 2.1 copy-start.9
  168.0 2.1 copy-start.9
  171.6 2.1 copy-start.9
  175.2 2.1 copy-start.9
  178.8 2.1 copy-start.9
  182.4 2.1 copy-start.9
  186.0 4.0 %copy-start.3 = (bf16[16,256,256]{2,1,0:T(8,128)(2,1)S(1)}, bf16[16,256,256]{2,1,0:T(8,128)(2,1)}, u32[]{:S(2)}) copy-start(bf16[16,256,256]{2,1,0:T(8,128)(2,1)} %get-tuple-element.54) | copy-start | bytes 6291460
  243.9 0.9 copy-start.6
  245.5 1.3 copy-start.2
  246.9 6.2 %collective-permute-start.2 = (bf16[2,384,256]{2,1,0:T(8,128)(2,1)S(1)}, bf16[2,384,256]{2,1,0:T(8,128)(2,1)S(1)}, u32[]{:S(2)}, u32[]{:S(2)}) collective-permute-start(bf16[2,384,256]{2,1,0:T(8,128)(2,1)S(1)} %get-tuple-element.112), channel_id=1, source_target_pairs={{0,1},{1,2},{2,3},{3,4},{4,5},{5,6},{6,7},{7,8},{8,9},{9,10},{10,1... | collective-permute-start | bytes 1179656 | tf_op jit(solution)/shard_map/ppermute | solution.py:15
  248.3 10.5 %collective-permute-start.3 = (bf16[2,384,256]{2,1,0:T(8,128)(2,1)S(1)}, bf16[2,384,256]{2,1,0:T(8,128)(2,1)S(1)}, u32[]{:S(2)}, u32[]{:S(2)}) collective-permute-start(bf16[2,384,256]{2,1,0:T(8,128)(2,1)S(1)} %get-tuple-element.113), channel_id=1, source_target_pairs={{1,0},{2,1},{3,2},{4,3},{5,4},{6,5},{7,6},{8,7},{9,8},{10,9},{11,1... | collective-permute-start | bytes 1179656 | tf_op jit(solution)/shard_map/ppermute | solution.py:18
  303.8 6.8 %copy-start.1 = (bf16[2,2048,256]{2,1,0:T(8,128)(2,1)S(1)}, bf16[2,2048,256]{2,1,0:T(8,128)(2,1)}, u32[]{:S(2)}) copy-start(bf16[2,2048,256]{2,1,0:T(8,128)(2,1)} %param.15) | copy-start | bytes 6291460
